TPU v7x, 32 devices: a whole 2x2x4 slice. The times are simulated.
32 devices in a mesh: ba: 8 (over z, x), ka: 4 (over y, core).
Axes of the slice: x: 2, y: 2, z: 4, core: 2. Of those that a mesh axis runs over, the one named last changes fastest.
Arguments:
- emb_one: bfloat16 [8192, 128], P('ba'), may hold values from -8 to 8, as said below
- emb_two: bfloat16 [8192, 128], P('ba'), may hold values from -8 to 8, as said below
- prototypes: float32 [3000, 128], P('ka', 'ba'), may hold values from -6 to 6, as said below
Outputs:
- assignment_weights: float32 [8192, 3000], P('ba', 'ka')
- row_loss: float32 [8192], P('ba')
Inputs may be any that keep to these rules, and one draw needn't show every extreme that they name: `prototypes`: prototype entries are finite and lie within the stated range. `emb_one`: embedding entries are finite and lie within the stated range; rows are not zero. `emb_two`: embedding entries are finite and lie within the stated range; rows are not zero.
All inputs are finite; a program needn't handle non-finite values.
Results may differ from a plain program's by a relative error of at most 0.0003.
Values sent between devices are 32-bit elements.
A program may use at most 64 MiB of HBM per device.

v0:
```python
import jax
import jax.numpy as jnp
from jax import lax
from jax.sharding import PartitionSpec as P

K = 3000
REPEAT_COUNT = 3


TEMP_CODE = 0.05
TEMP_PRED = 0.1


def unit_rows(values):
    values = values.astype(jnp.float32)
    factor = lax.rsqrt(jnp.sum(values * values, axis=1, keepdims=True))
    return (values * factor).astype(jnp.bfloat16)


def vector_columns(current):
    kernel, col_scale, row_scale = current
    return (
        jnp.sum(kernel[0] * row_scale[0][:, None], axis=0),
        jnp.sum(kernel[1] * row_scale[1][:, None], axis=0),
    )


def vector_by_columns(current, totals):
    return (current[0], (1.0 / totals[0], 1.0 / totals[1]), current[2])


def vector_samples(current):
    kernel, col_scale, row_scale = current
    return (
        jnp.sum(kernel[0] * col_scale[0][None, :], axis=1),
        jnp.sum(kernel[1] * col_scale[1][None, :], axis=1),
    )


def vector_by_samples(current, totals):
    return (current[0], current[1], (1.0 / totals[0], 1.0 / totals[1]))


def vector_raw(current):
    kernel, col_scale, row_scale = current
    return (
        kernel[0] * col_scale[0][None, :] * row_scale[0][:, None],
        kernel[1] * col_scale[1][None, :] * row_scale[1][:, None],
    )


def body(emb_one, emb_two, prototypes):
    gathered = lax.all_gather(prototypes, "ba", axis=1, tiled=True)
    centers = unit_rows(gathered)
    first_view_logits = jnp.dot(unit_rows(emb_one), centers.T, preferred_element_type=jnp.float32)
    second_view_logits = jnp.dot(unit_rows(emb_two), centers.T, preferred_element_type=jnp.float32)
    kernel = (jnp.exp(first_view_logits / TEMP_CODE), jnp.exp(second_view_logits / TEMP_CODE))
    column_part, column_apply = (vector_columns, vector_by_columns)
    sample_part, sample_apply, raw_matrix = (vector_samples, vector_by_samples, vector_raw)
    col_ones = jnp.ones((first_view_logits.shape[1],), jnp.float32)
    row_ones = jnp.ones((first_view_logits.shape[0],), jnp.float32)
    current = (kernel, (col_ones, col_ones), (row_ones, row_ones))
    for iteration in range(REPEAT_COUNT):
        partial_sums = column_part(current)
        totals = lax.psum((partial_sums[0], partial_sums[1]), "ba")
        current = column_apply(current, totals)
        if iteration + 1 < REPEAT_COUNT:
            partial_sums = sample_part(current)
            totals = lax.psum((partial_sums[0], partial_sums[1]), "ka")
            current = sample_apply(current, totals)
    raw_one, raw_two = raw_matrix(current)
    logit_one = first_view_logits / TEMP_PRED
    logit_two = second_view_logits / TEMP_PRED
    masses = lax.psum((jnp.sum(raw_one, axis=1), jnp.sum(raw_two, axis=1)), "ka")
    first_view_assignment = raw_one / masses[0][:, None]
    second_view_assignment = raw_two / masses[1][:, None]
    peaks = lax.pmax((jnp.max(logit_one, axis=1), jnp.max(logit_two, axis=1)), "ka")
    terms = lax.psum(
        (
            jnp.sum(jnp.exp(logit_one - peaks[0][:, None]), axis=1),
            jnp.sum(jnp.exp(logit_two - peaks[1][:, None]), axis=1),
            jnp.sum(first_view_assignment * logit_two, axis=1),
            jnp.sum(second_view_assignment * logit_one, axis=1),
        ),
        "ka",
    )
    lse_one = peaks[0] + jnp.log(terms[0])
    lse_two = peaks[1] + jnp.log(terms[1])
    row_loss = lse_two - terms[2] + lse_one - terms[3]
    return (K * first_view_assignment, row_loss)


def solution(mesh):
    placed = (P("ba", None), P("ba", None), P("ka", "ba"))
    return jax.shard_map(
        body, mesh=mesh, in_specs=placed, out_specs=(P("ba", "ka"), P("ba")), check_vma=False
    )
```

profile of v0, /device:TPU:0, one launch (start us, length us, event | category | flops | bytes accessed | tf_op | source)
XLA Modules:
  0.0 154.9 jit_solution(16839468313270747781)
XLA Ops:
  0.6 0.0 copy-start.1
  0.6 1.2 fusion.5
  1.9 1.2 fusion.7
  3.0 33.0 %all_gather.3 = f32[750,128]{0,1:T(8,128)S(1)} all-gather(f32[750,16]{0,1:T(8,128)} %param.5), channel_id=1, replica_groups=mesh['ba'=8,'ka'=4] {'ba'}, dimensions={1}, use_global_device_ids=true | all-gather | bytes 432000 | tf_op jit(solution)/shard_map/all_gather | solution.py:53
  36.1 1.8 %fusion.3 = (f32[750]{0:T(1024)S(1)}, f32[1024,750]{0,1:T(8,128)S(1)}) fusion(f32[750,128]{0,1:T(8,128)S(1)} %all_gather.3, f32[750]{0:T(1024)S(1)} %rsqrt.25, bf16[1024,128]{1,0:T(8,128)(2,1)} %param.3, f32[1024]{0:T(1024)S(1)} %rsqrt.24), kind=kOutput, calls=%fused_computation.22 | convolution fusion | flops 198728464 | bytes 3728240 | tf_op jit(solution)/shard_map/dot_general | solution.py:55
  37.9 0.0 copy-done.1
  37.9 2.6 %multiply_reduce_fusion.11 = (f32[1024]{0:T(1024)S(1)}, f32[750]{0:T(1024)S(1)}, f32[1024,750]{0,1:T(8,128)}) fusion(f32[750,128]{0,1:T(8,128)S(1)} %all_gather.3, f32[750]{0:T(1024)S(1)} %rsqrt.25, bf16[1024,128]{1,0:T(8,128)(2,1)S(1)} %copy-done.1, f32[1024]{0:T(1024)S(1)} %rsqrt.26), kind=kOutput, calls=%fused_computation.20 | convolution fusion | flops 200263440 | bytes 3732336 | tf_op jit(solution)/shard_map/dot_general | solution.py:56
  40.4 21.7 %all-reduce.2 = (f32[750]{0:T(1024)S(1)}, f32[750]{0:T(1024)S(1)}) all-reduce(f32[750]{0:T(1024)S(1)} %get-tuple-element.30, f32[750]{0:T(1024)S(1)} %get-tuple-element.7), channel_id=1, replica_groups=mesh['ba'=8,'ka'=4] {'ba'}, use_global_device_ids=true, to_apply=%region_3.0 | all-reduce | flops 1500 | bytes 12000 | tf_op jit(solution)/shard_map/psum | solution.py:65
  62.1 0.7 multiply_reduce_fusion.10
  62.9 5.8 %all-reduce.7 = (f32[1024]{0:T(1024)S(1)}, f32[1024]{0:T(1024)S(1)}) all-reduce(f32[1024]{0:T(1024)S(1)} %get-tuple-element.6, f32[1024]{0:T(1024)S(1)} %get-tuple-element.9), channel_id=1, replica_groups=mesh['ba'=8,'ka'=4] {'ka'}, use_global_device_ids=true, to_apply=%region_16.0 | all-reduce | flops 2048 | bytes 16384 | tf_op jit(solution)/shard_map/pmax | solution.py:77
  68.6 2.9 %exponential_reduce_fusion.1 = (f32[1024]{0:T(1024)S(1)}, f32[1024]{0:T(1024)S(1)}) fusion(f32[1024,750]{0,1:T(8,128)} %get-tuple-element.32, f32[1024]{0:T(1024)S(1)} %get-tuple-element.27, f32[750]{0:T(1024)S(1)} %broadcast_divide_fusion.6), kind=kLoop, calls=%fused_computation.9 | loop fusion | flops 4605952 | bytes 3087288 | tf_op jit(solution)/shard_map/reduce_sum | solution.py:81
  71.5 6.7 %all-reduce.6 = (f32[1024]{0:T(1024)S(1)}, f32[1024]{0:T(1024)S(1)}) all-reduce(f32[1024]{0:T(1024)S(1)} %get-tuple-element.10, f32[1024]{0:T(1024)S(1)} %get-tuple-element.5), channel_id=1, replica_groups=mesh['ba'=8,'ka'=4] {'ka'}, use_global_device_ids=true, to_apply=%region_5.0 | all-reduce | flops 2048 | bytes 16384 | tf_op jit(solution)/shard_map/psum | solution.py:69
  78.3 2.4 %multiply_reduce_fusion.3 = f32[750]{0:T(1024)S(1)} fusion(f32[1024]{0:T(1024)S(1)} %get-tuple-element.33, f32[1024,750]{0,1:T(8,128)} %get-tuple-element.32), kind=kLoop, calls=%fused_computation.4 | loop fusion | flops 2303250 | bytes 3079096 | tf_op jit(solution)/shard_map/reduce_sum | solution.py:24
  80.7 0.6 multiply_reduce_fusion.8
  81.3 17.4 %all-reduce.1 = (f32[750]{0:T(1024)S(1)}, f32[750]{0:T(1024)S(1)}) all-reduce(f32[750]{0:T(1024)S(1)} %multiply_reduce_fusion.8, f32[750]{0:T(1024)S(1)} %multiply_reduce_fusion.3), channel_id=1, replica_groups=mesh['ba'=8,'ka'=4] {'ba'}, use_global_device_ids=true, to_apply=%region_7.0 | all-reduce | flops 1500 | bytes 12000 | tf_op jit(solution)/shard_map/psum | solution.py:65
  98.7 0.0 copy-start
  98.7 0.5 multiply_reduce_fusion.7
  99.3 1.3 copy-done
  100.6 0.5 multiply_reduce_fusion.2
  101.1 5.8 %all-reduce.5 = (f32[1024]{0:T(1024)S(1)}, f32[1024]{0:T(1024)S(1)}) all-reduce(f32[1024]{0:T(1024)S(1)} %multiply_reduce_fusion.7, f32[1024]{0:T(1024)S(1)} %multiply_reduce_fusion.2), channel_id=1, replica_groups=mesh['ba'=8,'ka'=4] {'ka'}, use_global_device_ids=true, to_apply=%region_9.0 | all-reduce | flops 2048 | bytes 16384 | tf_op jit(solution)/shard_map/psum | solution.py:69
  106.9 2.4 %multiply_reduce_fusion.1 = f32[750]{0:T(1024)S(1)} fusion(f32[1024]{0:T(1024)S(1)} %broadcast_divide_fusion, f32[1024,750]{0,1:T(8,128)} %get-tuple-element.32), kind=kLoop, calls=%fused_computation.2 | loop fusion | flops 2303250 | bytes 3079096 | tf_op jit(solution)/shard_map/reduce_sum | solution.py:24
  109.4 0.6 multiply_reduce_fusion.6
  109.9 19.4 %all-reduce = (f32[750]{0:T(1024)S(1)}, f32[750]{0:T(1024)S(1)}) all-reduce(f32[750]{0:T(1024)S(1)} %multiply_reduce_fusion.6, f32[750]{0:T(1024)S(1)} %multiply_reduce_fusion.1), channel_id=1, replica_groups=mesh['ba'=8,'ka'=4] {'ba'}, use_global_device_ids=true, to_apply=%region_11.0 | all-reduce | flops 1500 | bytes 12000 | tf_op jit(solution)/shard_map/psum | solution.py:65
  129.3 2.5 %fusion.2 = f32[1024]{0:T(1024)S(1)} fusion(f32[750]{0:T(1024)S(1)} %broadcast_divide_fusion.4, f32[1024]{0:T(1024)S(1)} %broadcast_divide_fusion, f32[1024,750]{0,1:T(8,128)} %get-tuple-element.32), kind=kLoop, calls=%fused_computation.18 | loop fusion | flops 3070976 | bytes 3083192 | tf_op jit(solution)/shard_map/reduce_sum | solution.py:74
  131.9 0.6 fusion.1
  132.5 5.8 %all-reduce.4 = (f32[1024]{0:T(1024)S(1)}, f32[1024]{0:T(1024)S(1)}) all-reduce(f32[1024]{0:T(1024)S(1)} %fusion.1, f32[1024]{0:T(1024)S(1)} %fusion.2), channel_id=1, replica_groups=mesh['ba'=8,'ka'=4] {'ka'}, use_global_device_ids=true, to_apply=%region_13.0 | all-reduce | flops 2048 | bytes 16384 | tf_op jit(solution)/shard_map/psum | solution.py:74
  138.3 5.4 %multiply_reduce_fusion.5 = (f32[1024]{0:T(1024)S(1)}, f32[1024]{0:T(1024)S(1)}, f32[1024]{0:T(1024)S(1)}, f32[1024,750]{0,1:T(8,128)}) fusion(f32[1024,750]{0,1:T(8,128)} %get-tuple-element.32, f32[1024]{0:T(1024)S(1)} %get-tuple-element.21, f32[1024]{0:T(1024)S(1)} %broadcast_divide_fusion.2, f32[750]{0:T(1024)S(1)} %broadcast_divide_fusion.7, ...), kind=kLoop, calls=%fused_computation.8 | loop fusion | flops 13052928 | bytes 9254768 | tf_op jit(solution)/shard_map/reduce_sum | solution.py:82
  143.7 10.6 %all-reduce.3 = (f32[1024]{0:T(1024)S(1)}, f32[1024]{0:T(1024)S(1)}, f32[1024]{0:T(1024)S(1)}, f32[1024]{0:T(1024)S(1)}) all-reduce(f32[1024]{0:T(1024)S(1)} %get-tuple-element.3, f32[1024]{0:T(1024)S(1)} %get-tuple-element.8, f32[1024]{0:T(1024)S(1)} %get-tuple-element.2, ...), channel_id=1, replica_groups=mesh['ba'=8,'ka'=4] {'ka'}, use_global_device_ids=true, to_apply=%region_38.0 | all-reduce | flops 4096 | bytes 32768 | tf_op jit(solution)/shard_map/psum | solution.py:78
  154.3 0.6 add_subtract_fusion
  (13 shorter events, 0.1 us)
Async XLA Ops:
  0.6 37.2 %copy-start.1 = (bf16[1024,128]{1,0:T(8,128)(2,1)S(1)}, bf16[1024,128]{1,0:T(8,128)(2,1)}, u32[]{:S(2)}) copy-start(bf16[1024,128]{1,0:T(8,128)(2,1)} %param.4) | copy-start | bytes 786436
  98.7 1.9 %copy-start = (f32[1024,750]{0,1:T(8,128)S(1)}, f32[1024,750]{0,1:T(8,128)}, u32[]{:S(2)}) copy-start(f32[1024,750]{0,1:T(8,128)} %get-tuple-element.32) | copy-start | bytes 9216004
where the time goes:
time: 155 us
  blocking collectives  126 us (81%)
  other arithmetic  22.3 us (14%)
  matrix products  4.32 us (3%)
    psum x3, blocking collectives, body(): totals = lax.psum((partial_sums[0], partial_sums[1]), 'ba')  58.4 us
    all_gather x1, blocking collectives, body(): gathered = lax.all_gather(prototypes, 'ba', axis=1, tiled=True)  33 us
    psum x2, blocking collectives, body(): totals = lax.psum((partial_sums[0], partial_sums[1]), 'ka')  12.5 us
    psum x1, blocking collectives, body(): lax.psum((jnp.sum(jnp.exp(logit_one - peaks[0][:, None]), axis=1), jnp.su...  10.6 us
    pmax x1, blocking collectives, body(): lax.pmax((jnp.max(logit_one, axis=1), jnp.max(logit_two, axis=1)), 'ka')  5.77 us
    psum x1, blocking collectives, body(): lax.psum((jnp.sum(raw_one, axis=1), jnp.sum(raw_two, axis=1)), 'ka')  5.77 us
    reduce_sum x1, other arithmetic, body(): jnp.sum(first_view_assignment * logit_two, axis=1)  5.44 us
    reduce_sum x2, other arithmetic, vector_columns(): jnp.sum(kernel[1] * row_scale[1][:, None], axis=0)  4.9 us

commit v1 on v0

v1 whole, which is shorter than its diff:
```python
import functools

import jax
import jax.numpy as jnp
from jax import lax
from jax.experimental import pallas as pl
from jax.experimental.pallas import tpu as pltpu
from jax.sharding import PartitionSpec as P

REPEAT_COUNT = 3
TEMP_CODE = 0.05
TEMP_PRED = 0.1
LANES = 128
VMEM_LIMIT = 48 * 1024 * 1024
MESH = pl.DeviceIdType.MESH


def unit(values):
    values = values.astype(jnp.float32)
    return (values * lax.rsqrt(jnp.sum(values * values, axis=1, keepdims=True))).astype(jnp.bfloat16)


def fold_rows(tile):
    return jnp.sum(tile.T, axis=0, keepdims=True)


def balance_kernel(
    nba, nka, width,
    one_ref, two_ref, proto_ref,
    unit_ref, centers_ref, scale_ref, mass_ref, loss_ref,
    units, gathered, scores, codes, dens, row_scale,
    col_out, col_in, row_out, row_in, last_out, last_in,
    gather_send, gather_recv, col_send, col_recv, row_send, row_recv, last_send, last_recv,
):
    mine_ba = lax.axis_index("ba")
    mine_ka = lax.axis_index("ka")
    rows = one_ref.shape[0]
    blocks = rows // LANES
    feat = proto_ref.shape[0]
    padded = centers_ref.shape[1]
    tiles = padded // LANES
    ba_peer = [lax.rem(mine_ba + d, nba) for d in range(nba)]
    ka_peer = [lax.rem(mine_ka + d, nka) for d in range(nka)]

    barrier = pltpu.get_barrier_semaphore()
    for d in range(1, nba):
        pl.semaphore_signal(barrier, inc=1, device_id={"ba": ba_peer[d]}, device_id_type=MESH)
    for d in range(1, nka):
        pl.semaphore_signal(barrier, inc=1, device_id={"ka": ka_peer[d]}, device_id_type=MESH)
    pl.semaphore_wait(barrier, nba + nka - 2)

    pending = []

    def send(src, dst, send_sem, recv_sem, peer):
        copy = pltpu.make_async_remote_copy(
            src_ref=src, dst_ref=dst, send_sem=send_sem, recv_sem=recv_sem,
            device_id=peer, device_id_type=MESH,
        )
        copy.start()
        pending.append(copy)
        return copy

    gathers = [
        send(proto_ref, gathered.at[mine_ba], gather_send.at[d], gather_recv.at[d], {"ba": ba_peer[d]})
        for d in range(1, nba)
    ]
    gathered[mine_ba] = proto_ref[...]

    def norm_block(b, carry):
        at = pl.ds(pl.multiple_of(b * LANES, LANES), LANES)
        units[0, at, :] = unit(one_ref[at, :])
        units[1, at, :] = unit(two_ref[at, :])
        return carry

    lax.fori_loop(0, blocks, norm_block, 0)
    for copy in gathers:
        copy.wait_recv()
    whole = jnp.concatenate([gathered[b] for b in range(nba)], axis=0)
    factor = lax.rsqrt(jnp.sum(whole * whole, axis=0, keepdims=True))
    centers_ref[...] = jnp.zeros_like(centers_ref)
    centers_ref[:, :width] = (whole * factor).astype(jnp.bfloat16)

    valid = lax.broadcasted_iota(jnp.int32, (1, padded), 1) < width

    def lane(t):
        return slice(t * LANES, (t + 1) * LANES)

    def to_sublanes(acc):
        return jnp.concatenate([jnp.sum(a, axis=0, keepdims=True) for a in acc], axis=1)

    def fold8(tile):
        return jnp.sum(tile.reshape(LANES // 8, 8, LANES), axis=0)

    def first_pass(v):
        def step(b, acc):
            at = pl.ds(pl.multiple_of(b * LANES, LANES), LANES)
            score = jnp.dot(units[v, at, :], centers_ref[...], preferred_element_type=jnp.float32)
            scores[v, at, :] = score
            den = jnp.zeros((LANES, LANES), jnp.float32)
            out = []
            for t in range(tiles):
                soft = jnp.exp(score[:, lane(t)] * (1.0 / TEMP_PRED))
                if (t + 1) * LANES > width:
                    soft = jnp.where(valid[:, lane(t)], soft, 0.0)
                code = soft * soft
                codes[v, at, lane(t)] = code
                den = den + soft
                out.append(acc[t] + fold8(code))
            last_out[v, 2, pl.ds(b, 1), :] = fold_rows(den)
            return tuple(out)

        zero = tuple(jnp.zeros((8, LANES), jnp.float32) for _ in range(tiles))
        return to_sublanes(lax.fori_loop(0, blocks, step, zero))

    def column_pass(v):
        def step(b, acc):
            at = pl.ds(pl.multiple_of(b * LANES, LANES), LANES)
            weight = jnp.broadcast_to(row_scale[v, pl.ds(b, 1), :], (LANES, LANES)).T
            return tuple(acc[t] + fold8(codes[v, at, lane(t)] * weight) for t in range(tiles))

        zero = tuple(jnp.zeros((8, LANES), jnp.float32) for _ in range(tiles))
        return to_sublanes(lax.fori_loop(0, blocks, step, zero))

    def row_pass(v, scale, put):
        def step(b, carry):
            at = pl.ds(pl.multiple_of(b * LANES, LANES), LANES)
            acc = jnp.zeros((LANES, LANES), jnp.float32)
            for t in range(tiles):
                acc = acc + codes[v, at, lane(t)] * scale[:, lane(t)]
            put[pl.ds(b, 1), :] = fold_rows(acc)
            return carry

        lax.fori_loop(0, blocks, step, 0)

    def last_pass(v, scale):
        def step(b, carry):
            at = pl.ds(pl.multiple_of(b * LANES, LANES), LANES)
            mass = jnp.zeros((LANES, LANES), jnp.float32)
            cross = jnp.zeros((LANES, LANES), jnp.float32)
            for t in range(tiles):
                raw = codes[v, at, lane(t)] * scale[:, lane(t)]
                mass = mass + raw
                cross = cross + raw * scores[1 - v, at, lane(t)]
            last_out[v, 0, pl.ds(b, 1), :] = fold_rows(mass)
            last_out[v, 1, pl.ds(b, 1), :] = fold_rows(cross) * (1.0 / TEMP_PRED)
            return carry

        lax.fori_loop(0, blocks, step, 0)

    def send_columns(r, v, part):
        col_out[r, v] = part
        return [
            send(col_out.at[r, v], col_in.at[r, v, d], col_send.at[r, v, d], col_recv.at[r, v, d],
                 {"ba": ba_peer[d]})
            for d in range(1, nba)
        ]

    def send_samples(r, v):
        return [
            send(row_out.at[r, v], row_in.at[r, v, d], row_send.at[r, v, d], row_recv.at[r, v, d],
                 {"ka": ka_peer[d]})
            for d in range(1, nka)
        ]

    def column_scale(r, v, copies):
        total = col_out[r, v]
        for d in range(1, nba):
            copies[d - 1].wait_recv()
            total = total + col_in[r, v, d]
        return jnp.where(valid, 1.0 / total, 0.0)

    cols = [send_columns(0, v, first_pass(v)) for v in range(2)]
    for r in range(REPEAT_COUNT - 1):
        samples = []
        for v in range(2):
            row_pass(v, column_scale(r, v, cols[v]), row_out.at[r, v])
            samples.append(send_samples(r, v))
        cols = []
        for v in range(2):
            total = row_out[r, v]
            for d in range(1, nka):
                samples[v][d - 1].wait_recv()
                total = total + row_in[r, v, d]
            row_scale[v] = 1.0 / total
            cols.append(send_columns(r + 1, v, column_pass(v)))
    finals = []
    for v in range(2):
        scale = column_scale(REPEAT_COUNT - 1, v, cols[v])
        if v == 0:
            scale_ref[...] = scale
        last_pass(v, scale)
        finals.append([
            send(last_out.at[v], last_in.at[v, d], last_send.at[v, d], last_recv.at[v, d],
                 {"ka": ka_peer[d]})
            for d in range(1, nka)
        ])
    unit_ref[...] = units[0]
    loss = jnp.zeros(loss_ref.shape, jnp.float32)
    for v in range(2):
        mass, cross, den = last_out[v, 0], last_out[v, 1], last_out[v, 2]
        for d in range(1, nka):
            finals[v][d - 1].wait_recv()
            mass = mass + last_in[v, d, 0]
            cross = cross + last_in[v, d, 1]
            den = den + last_in[v, d, 2]
        if v == 0:
            mass_ref[...] = mass
        loss = loss + jnp.log(den) - cross / mass
    loss_ref[...] = loss
    for copy in pending:
        copy.wait_send()


def write_kernel(count, unit_ref, centers_ref, scale_ref, mass_ref, out_ref):
    step = pl.program_id(0)
    width = out_ref.shape[1]
    for b in range(out_ref.shape[0] // LANES):
        at = slice(b * LANES, (b + 1) * LANES)
        score = jnp.dot(unit_ref[at, :], centers_ref[...], preferred_element_type=jnp.float32)
        mass = mass_ref[pl.ds(step * (out_ref.shape[0] // LANES) + b, 1), :]
        weight = jnp.broadcast_to(count / mass, (LANES, LANES)).T
        for t in range(0, centers_ref.shape[1], LANES):
            end = min(t + LANES, width)
            soft = jnp.exp(score[:, t:end] * (1.0 / TEMP_PRED))
            out_ref[at, t:end] = soft * soft * scale_ref[:, t:end] * weight[:, : end - t]


def body(nba, nka, emb_one, emb_two, prototypes):
    rows, depth = emb_one.shape
    width, feat = prototypes.shape
    padded = -(-width // LANES) * LANES
    blocks = rows // LANES
    f32 = jnp.float32
    vmem = pl.BlockSpec(memory_space=pltpu.VMEM)
    dma = pltpu.SemaphoreType.DMA
    units, centers, scale, mass, loss = pl.pallas_call(
        functools.partial(balance_kernel, nba, nka, width),
        out_shape=(
            jax.ShapeDtypeStruct((rows, depth), jnp.bfloat16),
            jax.ShapeDtypeStruct((depth, padded), jnp.bfloat16),
            jax.ShapeDtypeStruct((1, padded), f32),
            jax.ShapeDtypeStruct((blocks, LANES), f32),
            jax.ShapeDtypeStruct((blocks, LANES), f32),
        ),
        in_specs=[vmem] * 3,
        out_specs=[vmem] * 5,
        scratch_shapes=[
            pltpu.VMEM((2, rows, depth), jnp.bfloat16),
            pltpu.VMEM((nba, feat, width), f32),
            pltpu.VMEM((2, rows, padded), f32),
            pltpu.VMEM((2, rows, padded), f32),
            pltpu.VMEM((8, LANES), f32),
            pltpu.VMEM((2, blocks, LANES), f32),
            pltpu.VMEM((REPEAT_COUNT, 2, 1, padded), f32),
            pltpu.VMEM((REPEAT_COUNT, 2, nba, 1, padded), f32),
            pltpu.VMEM((REPEAT_COUNT - 1, 2, blocks, LANES), f32),
            pltpu.VMEM((REPEAT_COUNT - 1, 2, nka, blocks, LANES), f32),
            pltpu.VMEM((2, 3, blocks, LANES), f32),
            pltpu.VMEM((2, nka, 3, blocks, LANES), f32),
            dma((nba,)), dma((nba,)),
            dma((REPEAT_COUNT, 2, nba)), dma((REPEAT_COUNT, 2, nba)),
            dma((REPEAT_COUNT - 1, 2, nka)), dma((REPEAT_COUNT - 1, 2, nka)),
            dma((2, nka)), dma((2, nka)),
        ],
        compiler_params=pltpu.CompilerParams(
            collective_id=0, has_side_effects=True, vmem_limit_bytes=VMEM_LIMIT
        ),
    )(emb_one, emb_two, prototypes.T)
    chunk = 2 * LANES if rows % (2 * LANES) == 0 else LANES
    weights = pl.pallas_call(
        functools.partial(write_kernel, float(width * nka)),
        grid=(rows // chunk,),
        out_shape=jax.ShapeDtypeStruct((rows, width), f32),
        in_specs=[
            pl.BlockSpec((chunk, depth), lambda i: (i, 0)),
            pl.BlockSpec((depth, padded), lambda i: (0, 0)),
            pl.BlockSpec((1, padded), lambda i: (0, 0)),
            pl.BlockSpec((blocks, LANES), lambda i: (0, 0)),
        ],
        out_specs=pl.BlockSpec((chunk, width), lambda i: (i, 0)),
    )(units, centers, scale, mass)
    return weights, loss.reshape(rows)


def solution(mesh):
    placed = (P("ba", None), P("ba", None), P("ka", "ba"))
    return jax.shard_map(
        functools.partial(body, mesh.shape["ba"], mesh.shape["ka"]),
        mesh=mesh, in_specs=placed, out_specs=(P("ba", "ka"), P("ba")), check_vma=False,
    )
```

time: 155 us -> 63 us (0.41)
  blocking collectives: 126 us -> 0 us
  Pallas kernels: 0 us -> 52.6 us
  other arithmetic: 22.3 us -> 0 us
  local copies, waits for them, and re-layouts: 1.32 us -> 9.34 us
  matrix products: 4.32 us -> 0 us
    psum x7 -> x0, blocking collectives: 87.3 us -> none  [the longest x3 58.4 us: body(): totals = lax.psum((partial_sums[0], partial_sums[1]), 'ba')]
    pallas_call x0 -> x2, Pallas kernels: none -> 52.6 us  [the longest x1 48.4 us: body(): pl.pallas_call(functools.partial(balance_kernel, nba, nka, width), out_sh...]
    all_gather x1 -> x0, blocking collectives: 33 us -> none  [body(): gathered = lax.all_gather(prototypes, 'ba', axis=1, tiled=True)]
    reduce_sum x13 -> x0, other arithmetic: 21 us -> none  [the longest x1 5.44 us: body(): jnp.sum(first_view_assignment * logit_two, axis=1)]
    unnamed x4 -> x16, local copies, waits for them, and re-layouts: 1.31 us -> 9.34 us
    pmax x1 -> x0, blocking collectives: 5.77 us -> none  [body(): lax.pmax((jnp.max(logit_one, axis=1), jnp.max(logit_two, axis=1)), 'ka')]
    dot_general x2 -> x0, matrix products: 4.32 us -> none  [the longest x1 2.57 us: body(): jnp.dot(unit_rows(emb_two), centers.T, preferred_element_type=jnp.float32)]
where the time goes in v1:
time: 63 us; the launch traced here: 62.6 us
  Pallas kernels  52.6 us (83%)
  local copies, waits for them, and re-layouts  9.34 us (15%)
  between operations  0.66 us (1%)
    pallas_call x1, Pallas kernels, body(): pl.pallas_call(functools.partial(balance_kernel, nba, nka, width), out_sh...  48.4 us
    unnamed x16, local copies, waits for them, and re-layouts  9.34 us
    pallas_call x1, Pallas kernels, body(): pl.pallas_call(functools.partial(write_kernel, float(width * nka)), grid=...  4.21 us

profile of v1, /device:TPU:0, one launch (start us, length us, event | category | flops | bytes accessed | tf_op | source)
XLA Modules:
  0.0 62.6 jit_solution(10637665628671299699)
XLA Ops:
  0.6 0.0 copy-start.1
  0.6 0.9 %copy-done.1 = bf16[1024,128]{1,0:T(8,128)(2,1)S(1)} copy-done((bf16[1024,128]{1,0:T(8,128)(2,1)S(1)}, bf16[1024,128]{1,0:T(8,128)(2,1)}, u32[]{:S(2)}) %copy-start.1) | copy-done | bytes 262168
  1.6 0.0 copy-start.2
  1.6 0.9 %copy-done.2 = bf16[1024,128]{1,0:T(8,128)(2,1)S(1)} copy-done((bf16[1024,128]{1,0:T(8,128)(2,1)S(1)}, bf16[1024,128]{1,0:T(8,128)(2,1)}, u32[]{:S(2)}) %copy-start.2) | copy-done | bytes 262168
  2.5 0.0 copy-start.4
  2.5 0.8 %copy-done.4 = f32[750,16]{0,1:T(8,128)S(1)} copy-done((f32[750,16]{0,1:T(8,128)S(1)}, f32[750,16]{0,1:T(8,128)}, u32[]{:S(2)}) %copy-start.4) | copy-done | bytes 48024
  3.3 48.4 %shard_map.50 = (bf16[1024,128]{1,0:T(8,128)(2,1)S(1)}, bf16[128,768]{1,0:T(8,128)(2,1)S(1)}, f32[1,768]{1,0:T(1,128)S(1)}, f32[8,128]{1,0:T(8,128)S(1)}, f32[8,128]{1,0:T(8,128)S(1)}) custom-call(bf16[1024,128]{1,0:T(8,128)(2,1)S(1)} %copy-done.1, bf16[1024,128]{1,0:T(8,128)(2,1)S(1)} %copy-done.2, f32[16,750]{1,0:T(8,128)S(1)} %bitcast.2), custom_call_target="tpu_custom_call" | custom-call | tf_op jit(solution)/shard_map/pallas_call | solution.py:236
  51.8 0.0 copy-start
  51.8 0.7 %copy-done = bf16[1024,128]{1,0:T(8,128)(2,1)} copy-done((bf16[1024,128]{1,0:T(8,128)(2,1)}, bf16[1024,128]{1,0:T(8,128)(2,1)S(1)}, u32[]{:S(2)}) %copy-start) | copy-done | bytes 262168
  52.5 0.0 copy-start.3
  52.5 0.7 %copy-done.3 = bf16[128,768]{1,0:T(8,128)(2,1)} copy-done((bf16[128,768]{1,0:T(8,128)(2,1)}, bf16[128,768]{1,0:T(8,128)(2,1)S(1)}, u32[]{:S(2)}) %copy-start.3) | copy-done | bytes 196632
  53.1 0.0 copy-start.5
  53.1 0.6 copy-done.5
  53.7 0.0 copy-start.6
  53.7 0.6 copy-done.6
  54.3 4.2 %shard_map.51 = f32[1024,750]{1,0:T(8,128)} custom-call(bf16[1024,128]{1,0:T(8,128)(2,1)} %copy-done, bf16[128,768]{1,0:T(8,128)(2,1)} %copy-done.3, f32[1,768]{1,0:T(1,128)} %copy-done.6, f32[8,128]{1,0:T(8,128)} %copy-done.5), custom_call_target="tpu_custom_call" | custom-call | tf_op jit(solution)/shard_map/pallas_call | solution.py:270
  58.5 3.5 %copy.5 = f32[1024,750]{0,1:T(8,128)} copy(f32[1024,750]{1,0:T(8,128)} %shard_map.51) | data formatting | bytes 6144000
  62.0 0.6 copy.7
Async XLA Ops:
  0.6 1.0 %copy-start.1 = (bf16[1024,128]{1,0:T(8,128)(2,1)S(1)}, bf16[1024,128]{1,0:T(8,128)(2,1)}, u32[]{:S(2)}) copy-start(bf16[1024,128]{1,0:T(8,128)(2,1)} %one_ref.1) | copy-start | bytes 786436
  1.6 0.9 %copy-start.2 = (bf16[1024,128]{1,0:T(8,128)(2,1)S(1)}, bf16[1024,128]{1,0:T(8,128)(2,1)}, u32[]{:S(2)}) copy-start(bf16[1024,128]{1,0:T(8,128)(2,1)} %two_ref.1) | copy-start | bytes 786436
  2.5 0.8 %copy-start.4 = (f32[750,16]{0,1:T(8,128)S(1)}, f32[750,16]{0,1:T(8,128)}, u32[]{:S(2)}) copy-start(f32[750,16]{0,1:T(8,128)} %param.5) | copy-start | bytes 144004
  51.8 0.7 %copy-start = (bf16[1024,128]{1,0:T(8,128)(2,1)}, bf16[1024,128]{1,0:T(8,128)(2,1)S(1)}, u32[]{:S(2)}) copy-start(bf16[1024,128]{1,0:T(8,128)(2,1)S(1)} %get-tuple-element.7.unit_ref) | copy-start | bytes 786436
  52.5 0.7 %copy-start.3 = (bf16[128,768]{1,0:T(8,128)(2,1)}, bf16[128,768]{1,0:T(8,128)(2,1)S(1)}, u32[]{:S(2)}) copy-start(bf16[128,768]{1,0:T(8,128)(2,1)S(1)} %get-tuple-element.8.centers_ref) | copy-start | bytes 589828
  53.1 0.6 copy-start.5
  53.7 0.6 copy-start.6

commit v2 on v1

--- a/solution.py
+++ b/solution.py
@@ -11,7 +11,7 @@
 TEMP_CODE = 0.05
 TEMP_PRED = 0.1
 LANES = 128
-VMEM_LIMIT = 48 * 1024 * 1024
+VMEM_LIMIT = 67_043_328
 MESH = pl.DeviceIdType.MESH
 
 
@@ -26,9 +26,9 @@
 
 def balance_kernel(
     nba, nka, width,
-    one_ref, two_ref, proto_ref,
+    one_hbm, two_hbm, proto_hbm,
     unit_ref, centers_ref, scale_ref, mass_ref, loss_ref,
-    units, gathered, scores, codes, dens, row_scale,
+    one_ref, two_ref, proto_ref, units, gathered, scores, codes, row_scale, load_sem,
     col_out, col_in, row_out, row_in, last_out, last_in,
     gather_send, gather_recv, col_send, col_recv, row_send, row_recv, last_send, last_recv,
 ):
@@ -42,6 +42,12 @@
     ba_peer = [lax.rem(mine_ba + d, nba) for d in range(nba)]
     ka_peer = [lax.rem(mine_ka + d, nka) for d in range(nka)]
 
+    loads = [
+        pltpu.make_async_copy(src, dst, load_sem.at[i])
+        for i, (src, dst) in enumerate(((proto_hbm, proto_ref), (one_hbm, one_ref), (two_hbm, two_ref)))
+    ]
+    for load in loads:
+        load.start()
     barrier = pltpu.get_barrier_semaphore()
     for d in range(1, nba):
         pl.semaphore_signal(barrier, inc=1, device_id={"ba": ba_peer[d]}, device_id_type=MESH)
@@ -60,11 +66,23 @@
         pending.append(copy)
         return copy
 
+    pair = 2 if nba % 2 == 0 else 1
+    groups = nba // pair
+    group, side = mine_ba // pair, lax.rem(mine_ba, pair)
+    other = group * pair + (pair - 1 - side)
+    loads[0].wait()
     gathers = [
-        send(proto_ref, gathered.at[mine_ba], gather_send.at[d], gather_recv.at[d], {"ba": ba_peer[d]})
-        for d in range(1, nba)
+        send(proto_ref, gathered.at[mine_ba], gather_send.at[d], gather_recv.at[d],
+             {"ba": lax.rem(group + d, groups) * pair + side})
+        for d in range(1, groups)
     ]
+    crossed = []
+    if pair == 2:
+        crossed.append(send(proto_ref, gathered.at[mine_ba], gather_send.at[groups],
+                            gather_recv.at[groups], {"ba": other}))
     gathered[mine_ba] = proto_ref[...]
+    loads[1].wait()
+    loads[2].wait()
 
     def norm_block(b, carry):
         at = pl.ds(pl.multiple_of(b * LANES, LANES), LANES)
@@ -72,8 +90,18 @@
         units[1, at, :] = unit(two_ref[at, :])
         return carry
 
-    lax.fori_loop(0, blocks, norm_block, 0)
-    for copy in gathers:
+    order = sorted(range(1, groups), key=lambda d: min(d, groups - d))
+    share = -(-blocks // max(len(order), 1))
+    for place, d in enumerate(order):
+        gathers[d - 1].wait_recv()
+        if pair == 2:
+            owner = lax.rem(group + (groups - d), groups) * pair + side
+            crossed.append(send(gathered.at[owner], gathered.at[owner], gather_send.at[groups + d],
+                                gather_recv.at[groups + d], {"ba": other}))
+        lax.fori_loop(min(place * share, blocks), min((place + 1) * share, blocks), norm_block, 0)
+    if not order:
+        lax.fori_loop(0, blocks, norm_block, 0)
+    for copy in crossed:
         copy.wait_recv()
     whole = jnp.concatenate([gathered[b] for b in range(nba)], axis=0)
     factor = lax.rsqrt(jnp.sum(whole * whole, axis=0, keepdims=True))
@@ -211,18 +239,29 @@
         copy.wait_send()
 
 
-def write_kernel(count, unit_ref, centers_ref, scale_ref, mass_ref, out_ref):
-    step = pl.program_id(0)
-    width = out_ref.shape[1]
-    for b in range(out_ref.shape[0] // LANES):
-        at = slice(b * LANES, (b + 1) * LANES)
-        score = jnp.dot(unit_ref[at, :], centers_ref[...], preferred_element_type=jnp.float32)
-        mass = mass_ref[pl.ds(step * (out_ref.shape[0] // LANES) + b, 1), :]
-        weight = jnp.broadcast_to(count / mass, (LANES, LANES)).T
-        for t in range(0, centers_ref.shape[1], LANES):
-            end = min(t + LANES, width)
-            soft = jnp.exp(score[:, t:end] * (1.0 / TEMP_PRED))
-            out_ref[at, t:end] = soft * soft * scale_ref[:, t:end] * weight[:, : end - t]
+def write_kernel(
+    count, unit_ref, centers_ref, scale_ref, mass_ref, loss_ref, out_hbm, loss_out, out_ref, sem
+):
+    width, rows = out_ref.shape
+    copies = []
+    for start in range(0, width, LANES):
+        size = min(LANES, width - start)
+        tile = slice(start, start + LANES)
+        score = lax.dot_general(
+            centers_ref[:, tile], unit_ref[...], (((0,), (1,)), ((), ())), preferred_element_type=jnp.float32
+        )
+        weight = jnp.broadcast_to(scale_ref[:, tile] * count, (LANES, LANES)).T
+        for b in range(rows // LANES):
+            at = slice(b * LANES, (b + 1) * LANES)
+            soft = jnp.exp(score[:, at] * (1.0 / TEMP_PRED))
+            value = soft * soft * weight * (1.0 / mass_ref[b : b + 1, :])
+            out_ref[start : start + size, at] = value[:size]
+        part = pl.ds(start, size)
+        copies.append(pltpu.make_async_copy(out_ref.at[part], out_hbm.at[part], sem.at[len(copies)]))
+        copies[-1].start()
+    loss_out[...] = loss_ref[...]
+    for copy in copies:
+        copy.wait()
 
 
 def body(nba, nka, emb_one, emb_two, prototypes):
@@ -242,15 +281,18 @@
             jax.ShapeDtypeStruct((blocks, LANES), f32),
             jax.ShapeDtypeStruct((blocks, LANES), f32),
         ),
-        in_specs=[vmem] * 3,
+        in_specs=[pl.BlockSpec(memory_space=pltpu.HBM)] * 3,
         out_specs=[vmem] * 5,
         scratch_shapes=[
+            pltpu.VMEM((rows, depth), jnp.bfloat16),
+            pltpu.VMEM((rows, depth), jnp.bfloat16),
+            pltpu.VMEM((feat, width), f32),
             pltpu.VMEM((2, rows, depth), jnp.bfloat16),
             pltpu.VMEM((nba, feat, width), f32),
             pltpu.VMEM((2, rows, padded), f32),
             pltpu.VMEM((2, rows, padded), f32),
-            pltpu.VMEM((8, LANES), f32),
             pltpu.VMEM((2, blocks, LANES), f32),
+            dma((3,)),
             pltpu.VMEM((REPEAT_COUNT, 2, 1, padded), f32),
             pltpu.VMEM((REPEAT_COUNT, 2, nba, 1, padded), f32),
             pltpu.VMEM((REPEAT_COUNT - 1, 2, blocks, LANES), f32),
@@ -266,20 +308,17 @@
             collective_id=0, has_side_effects=True, vmem_limit_bytes=VMEM_LIMIT
         ),
     )(emb_one, emb_two, prototypes.T)
-    chunk = 2 * LANES if rows % (2 * LANES) == 0 else LANES
-    weights = pl.pallas_call(
+    weights, loss = pl.pallas_call(
         functools.partial(write_kernel, float(width * nka)),
-        grid=(rows // chunk,),
-        out_shape=jax.ShapeDtypeStruct((rows, width), f32),
-        in_specs=[
-            pl.BlockSpec((chunk, depth), lambda i: (i, 0)),
-            pl.BlockSpec((depth, padded), lambda i: (0, 0)),
-            pl.BlockSpec((1, padded), lambda i: (0, 0)),
-            pl.BlockSpec((blocks, LANES), lambda i: (0, 0)),
-        ],
-        out_specs=pl.BlockSpec((chunk, width), lambda i: (i, 0)),
-    )(units, centers, scale, mass)
-    return weights, loss.reshape(rows)
+        out_shape=(
+            jax.ShapeDtypeStruct((width, rows), f32),
+            jax.ShapeDtypeStruct((blocks, LANES), f32),
+        ),
+        in_specs=[vmem] * 5,
+        out_specs=(pl.BlockSpec(memory_space=pltpu.HBM), vmem),
+        scratch_shapes=[pltpu.VMEM((width, rows), f32), dma((padded // LANES,))],
+    )(units, centers, scale, mass, loss)
+    return weights.T, loss.reshape(rows)
 
 
 def solution(mesh):

time: 63 us -> 52.1 us (0.83)
  local copies, waits for them, and re-layouts: 9.34 us -> 0 us
  Pallas kernels: 52.6 us -> 51.4 us
    unnamed x16 -> x0, local copies, waits for them, and re-layouts: 9.34 us -> none
    pallas_call x1, Pallas kernels: 48.4 us -> 47.7 us  [body(): pl.pallas_call(functools.partial(balance_kernel, nba, nka, width), out_sh...]
where the time goes in v2:
time: 52.1 us; the launch traced here: 52 us
  Pallas kernels  51.4 us (99%)
  between operations  0.64 us (1%)
    pallas_call x1, Pallas kernels, body(): pl.pallas_call(functools.partial(balance_kernel, nba, nka, width), out_sh...  47.7 us
    pallas_call x1, Pallas kernels, body(): pl.pallas_call(functools.partial(write_kernel, float(width * nka)), out_s...  3.65 us

profile of v2, /device:TPU:0, one launch (start us, length us, event | category | flops | bytes accessed | tf_op | source)
XLA Modules:
  0.0 52.0 jit_solution(11517565691577663641)
XLA Ops:
  0.6 47.7 %shard_map.50 = (bf16[1024,128]{1,0:T(8,128)(2,1)}, bf16[128,768]{1,0:T(8,128)(2,1)}, f32[1,768]{1,0:T(1,128)}, f32[8,128]{1,0:T(8,128)}, f32[8,128]{1,0:T(8,128)}) custom-call(bf16[1024,128]{1,0:T(8,128)(2,1)} %one_hbm.1, bf16[1024,128]{1,0:T(8,128)(2,1)} %two_hbm.1, f32[16,750]{1,0:T(8,128)} %bitcast.3), custom_call_target="tpu_custom_call" | custom-call | tf_op jit(solution)/shard_map/pallas_call | solution.py:275
  48.3 3.6 %shard_map.51 = (f32[750,1024]{1,0:T(8,128)}, f32[8,128]{1,0:T(8,128)}) custom-call(bf16[1024,128]{1,0:T(8,128)(2,1)} %get-tuple-element.9.unit_ref, bf16[128,768]{1,0:T(8,128)(2,1)} %get-tuple-element.10.centers_ref, f32[1,768]{1,0:T(1,128)} %get-tuple-element.11.scale_ref, f32[8,128]{1,0:T(8,128)} %get-tuple-element.12.mass_ref, ...), custom_call_target="tpu_custom_call" | custom-call | tf_op jit(solution)/shard_map/pallas_call | solution.py:311
